TPU v7x, 32 devices: a whole 2x2x4 slice. The times are simulated.
32 devices in a mesh: gx: 8 (over y, x, core), gy: 4 (over z).
Axes of the slice: x: 2, y: 2, z: 4, core: 2. Of those that a mesh axis runs over, the one named last changes fastest.
Arguments:
- ocean_heat_field: float32 [8, 192, 128, 128], P('gy', 'gx'), may hold values from -6 to 6
- patch_zone: int32 [192], replicated, may hold values from 0 to 31, as said below
- patch_position: int32 [192], replicated, may hold values from 0 to 11, as said below
- quarter_spins: int32 [192], replicated, may hold values from 0 to 3
- zone_patch_tally: int32 [32], P(('gx', 'gy')), may hold values from 0 to 12, as said below
Outputs:
- regional: float32 [8, 32, 12, 128, 128], P(None, ('gx', 'gy'))
Inputs may be any that keep to these rules, and one draw needn't show every extreme that they name: In each aligned group of 24 blocks no more than 6 go to regions of one column patch_zone // 4, and each group has a column with exactly 6. A region receives at most 12 blocks and some region receives exactly 12. `patch_position`: the blocks of one region have distinct slots 0 to zone_patch_tally of that region minus 1, in increasing block order. zone_patch_tally[r] is the number of blocks j with patch_zone[j] = r.
All inputs are finite; a program needn't handle non-finite values.
Results may differ from a plain program's by a relative error of at most 0.00002.
Values sent between devices are 32-bit elements; how exact they have to be, the bound alone decides.
A program may use at most 128 MiB of HBM per device.

v0:
```python
import jax
import jax.numpy as jnp
from jax import lax
from jax.sharding import PartitionSpec as P


def spin_patches(incoming_patches, turn_codes):
    first_turn = jnp.rot90(incoming_patches, 1, axes=(2, 3))
    half_turn = jnp.rot90(incoming_patches, 2, axes=(2, 3))
    last_turn = jnp.rot90(incoming_patches, 3, axes=(2, 3))
    shaped = turn_codes[None, :, None, None]
    return jnp.where(
        shaped == 0,
        incoming_patches,
        jnp.where(shaped == 1, first_turn, jnp.where(shaped == 2, half_turn, last_turn)),
    )


def rank_within(labels, label_count):
    onehot = (labels[:, None] == jnp.arange(label_count, dtype=jnp.int32)[None, :]).astype(
        jnp.int32
    )
    running = jnp.cumsum(onehot, axis=0) - onehot
    return jnp.sum(running * onehot, axis=1)


def on_device(ocean_heat_field, patch_zone, patch_position, quarter_spins, zone_patch_tally):
    epoch_anomalies = ocean_heat_field.shape[0]
    patch_anomalies = ocean_heat_field.shape[1]
    patch_side_length = ocean_heat_field.shape[2]
    column_count = lax.axis_size("gx")
    row_count = lax.axis_size("gy")
    block_total = patch_zone.shape[0]
    per_peer = 2 * patch_anomalies // column_count
    capacity = 2 * patch_anomalies // row_count
    column = patch_zone // row_count
    block_ids = jnp.arange(block_total, dtype=jnp.int32)
    source_group = block_ids // patch_anomalies
    order_rank = rank_within(source_group * column_count + column, column_count * column_count)
    send_place = column * per_peer + order_rank
    my_column = lax.axis_index("gx")
    first_block = my_column * patch_anomalies
    mine_place = lax.dynamic_slice_in_dim(send_place, first_block, patch_anomalies)
    mine_turns = lax.dynamic_slice_in_dim(quarter_spins, first_block, patch_anomalies)
    incoming_patches = ocean_heat_field
    incoming_patches = spin_patches(incoming_patches, mine_turns)
    outgoing = jnp.zeros(
        (epoch_anomalies, column_count * per_peer, patch_side_length, patch_side_length),
        jnp.float32,
    )
    outgoing = outgoing.at[:, mine_place].set(incoming_patches)
    arrived = lax.all_to_all(outgoing, "gx", split_axis=1, concat_axis=1, tiled=True)
    arrival = source_group * per_peer + order_rank
    row_ids = jnp.arange(row_count, dtype=jnp.int32)[:, None]
    slot_ids = jnp.arange(capacity, dtype=jnp.int32)[None, :]
    targets = ((my_column * row_count + row_ids) * capacity + slot_ids).reshape(-1)
    flat_dest = patch_zone * capacity + patch_position
    matched = flat_dest[None, :] == targets[:, None]
    source = jnp.sum(jnp.where(matched, arrival[None, :] + 1, 0), axis=1) - 1
    present = source >= 0
    picked = jnp.take(arrived, jnp.maximum(source, 0), axis=1)
    picked = jnp.where(present[None, :, None, None], picked, jnp.float32(0.0))
    regional = lax.all_to_all(picked, "gy", split_axis=1, concat_axis=0, tiled=True)
    in_use = jnp.arange(capacity, dtype=jnp.int32) < zone_patch_tally[0]
    regional = jnp.where(in_use[None, :, None, None], regional, jnp.float32(0.0))
    regional = regional - jnp.mean(regional, axis=0, keepdims=True)
    return regional[:, None]


def solution(mesh):
    placed = (P("gy", "gx", None, None), P(), P(), P(), P(("gx", "gy")))
    return jax.shard_map(
        on_device,
        mesh=mesh,
        in_specs=placed,
        out_specs=P(None, ("gx", "gy"), None, None, None),
        check_vma=False,
    )
```

profile of v0, /device:TPU:2, one launch (start us, length us, event | category | flops | bytes accessed | tf_op | source)
XLA Modules:
  0.0 334.6 jit_solution(8710687670302286173)
XLA Ops:
  0.0 2.4 copy.42
  2.4 25.7 %rev.17 = f32[2,24,128,128]{3,2,1,0:T(8,128)} reverse(f32[2,24,128,128]{3,2,1,0:T(8,128)} %param.5), dimensions={2,3} | reverse | bytes 6291456 | tf_op jit(solution)/shard_map/jit(rot90)/jit(_flip)/rev | solution.py:9
  28.1 0.0 copy-start.2
  28.1 15.3 %rev.16 = f32[2,24,128,128]{2,3,1,0:T(8,128)} reverse(f32[2,24,128,128]{2,3,1,0:T(8,128)S(1)} %copy.42), dimensions={3} | reverse | bytes 6291456 | tf_op jit(solution)/shard_map/jit(rot90)/jit(_flip)/rev | solution.py:8
  43.4 17.0 %rev.18 = f32[2,24,128,128]{3,2,1,0:T(8,128)} reverse(f32[2,24,128,128]{3,2,1,0:T(8,128)S(1)} %bitcast.34), dimensions={3} | reverse | bytes 6291456 | tf_op jit(solution)/shard_map/jit(rot90)/jit(_flip)/rev | solution.py:10
  60.4 0.0 copy-done.2
  60.4 0.1 broadcast_compare_fusion.2
  60.5 6.2 %fusion.2 = f32[24,2,128,128]{3,2,0,1:T(8,128)S(1)} fusion(f32[2,24,128,128]{3,2,1,0:T(8,128)} %param.5, f32[2,24,128,128]{2,3,1,0:T(8,128)} %rev.16, f32[2,24,128,128]{3,2,1,0:T(8,128)} %rev.17, f32[2,24,128,128]{3,2,1,0:T(8,128)} %rev.18, pred[24]{0:T(512)(128)(4,1)S(1)} %get-tuple-element.12, pred[24]{0:T(512)(128)(4,1)S(1)} %get-tuple-element.11, ...), kind=kLoop, calls=%fused_computation.8 | loop fusion | flops 2359296 | bytes 15728712 | tf_op jit(solution)/shard_map/jit(_where)/select_n | solution.py:12
  66.7 0.0 copy-start
  66.7 0.0 copy-start.1
  66.7 0.2 copy.44
  66.9 0.4 copy-done
  67.4 0.0 copy-done.1
  67.4 0.6 reduce-window.6
  68.0 0.2 slice_reduce_fusion
  68.3 0.1 bitcast_bitcast_fusion
  68.4 0.1 compare_select_fusion
  68.5 3.5 %broadcast_in_dim.88 = f32[2,48,128,128]{3,2,1,0:T(8,128)} broadcast(f32[]{:T(128)} %constant.72.clone.1), dimensions={} | broadcast | bytes 6291460 | tf_op jit(solution)/shard_map/broadcast_in_dim | solution.py:47
  72.0 6.4 %scatter_fusion = f32[2,48,128,128]{3,2,1,0:T(8,128)} fusion(f32[2,48,128,128]{3,2,1,0:T(8,128)} %broadcast_in_dim.88, s32[24]{0:T(128)S(1)} %compare_select_fusion, f32[24,2,128,128]{3,2,1,0:T(8,128)S(1)} %copy.44), kind=kCustom, calls=%fused_computation.1 | custom fusion | bytes 9437280 | tf_op jit(solution)/shard_map/scatter | solution.py:51
  78.4 6.2 %copy.45 = f32[2,48,128,128]{3,2,0,1:T(8,128)} copy(f32[2,48,128,128]{3,2,1,0:T(8,128)} %scatter_fusion) | data formatting | bytes 12582912 | tf_op jit(solution)/shard_map/scatter | solution.py:51
  84.7 4.7 %all-to-all-start = ((f32[2,48,128,128]{3,2,0,1:T(8,128)}), f32[2,48,128,128]{3,2,0,1:T(8,128)}, u32[]{:S(2)}, u32[]{:S(2)}) async-start(f32[2,48,128,128]{3,2,0,1:T(8,128)} %copy.45), calls=%async_computation | async-start | bytes 12582912 | tf_op jit(solution)/shard_map/all_to_all | solution.py:52
  89.4 0.1 iota_add_fusion
  89.5 0.1 add.94
  89.6 0.2 select_reduce_fusion.1
  89.8 69.4 %all-to-all-done = f32[2,48,128,128]{3,2,0,1:T(8,128)} async-done(((f32[2,48,128,128]{3,2,0,1:T(8,128)}), f32[2,48,128,128]{3,2,0,1:T(8,128)}, u32[]{:S(2)}, u32[]{:S(2)}) %all-to-all-start) | async-done | bytes 6291488 | tf_op jit(solution)/shard_map/all_to_all | solution.py:52
  159.2 6.3 %copy.46 = f32[2,48,128,128]{3,2,1,0:T(8,128)} copy(f32[2,48,128,128]{3,2,0,1:T(8,128)} %all-to-all-done) | data formatting | bytes 12582912 | tf_op jit(solution)/shard_map/all_to_all | solution.py:52
  165.5 6.4 %gather_fusion = f32[48,2,128,128]{3,2,1,0:T(8,128)} fusion(f32[2,48,128,128]{3,2,1,0:T(8,128)} %copy.46, s32[1024]{0:T(1024)S(1)} %pad_clamp_fusion), kind=kCustom, calls=%fused_computation | custom fusion | bytes 12583104 | tf_op jit(solution)/shard_map/jit(_take)/gather | solution.py:61
  171.9 7.0 %select_bitcast_fusion = f32[2,48,128,128]{3,2,0,1:T(8,128)} fusion(f32[48,2,128,128]{3,2,1,0:T(8,128)} %gather_fusion, pred[48]{0:T(512)(128)(4,1)S(1)} %get-tuple-element.14, pred[48]{0:T(512)(128)(4,1)S(1)} %get-tuple-element.13), kind=kLoop, calls=%fused_computation.4 | loop fusion | flops 3145728 | bytes 12583008 | tf_op jit(solution)/shard_map/jit(_where)/select_n | solution.py:62
  178.9 5.7 %all-to-all-start.1 = ((f32[2,48,128,128]{3,2,0,1:T(8,128)}), f32[2,48,128,128]{3,2,0,1:T(8,128)}, u32[]{:S(2)}, u32[]{:S(2)}) async-start(f32[2,48,128,128]{3,2,0,1:T(8,128)} %select_bitcast_fusion), calls=%async_computation.1 | async-start | bytes 12582912 | tf_op jit(solution)/shard_map/all_to_all | solution.py:63
  185.2 138.3 %all-to-all-done.1 = f32[2,48,128,128]{3,2,0,1:T(8,128)} async-done(((f32[2,48,128,128]{3,2,0,1:T(8,128)}), f32[2,48,128,128]{3,2,0,1:T(8,128)}, u32[]{:S(2)}, u32[]{:S(2)}) %all-to-all-start.1) | async-done | bytes 6291488 | tf_op jit(solution)/shard_map/all_to_all | solution.py:63
  323.5 3.2 copy.47
  326.8 0.8 select_reduce_fusion
  327.5 0.1 broadcast_multiply_fusion
  327.6 3.2 copy.48
  330.8 3.7 %fusion = f32[8,1,12,128,128]{4,3,2,0,1:T(8,128)} fusion(f32[4,2,12,128,128]{4,3,2,1,0:T(8,128)S(1)} %copy.48, f32[12,128,128]{2,1,0:T(8,128)S(1)} %broadcast_multiply_fusion, pred[12]{0:T(512)(128)(4,1)S(1)} %iota_compare_fusion.2), kind=kLoop, calls=%fused_computation.3 | loop fusion | flops 3145728 | bytes 13369356 | tf_op jit(solution)/shard_map/sub | solution.py:66
  (12 shorter events, 0.2 us)
Async XLA Ops:
  28.1 32.4 %copy-start.2 = (s32[192]{0:T(256)S(1)}, s32[192]{0:T(256)}, u32[]{:S(2)}) copy-start(s32[192]{0:T(256)} %param.8) | copy-start | bytes 2308
  66.7 0.7 copy-start
  66.7 0.7 copy-start.1
  84.7 74.5 %all-to-all-start = ((f32[2,48,128,128]{3,2,0,1:T(8,128)}), f32[2,48,128,128]{3,2,0,1:T(8,128)}, u32[]{:S(2)}, u32[]{:S(2)}) async-start(f32[2,48,128,128]{3,2,0,1:T(8,128)} %copy.45), calls=%async_computation | async-start | bytes 12582912 | tf_op jit(solution)/shard_map/all_to_all | solution.py:52
  178.9 144.6 %all-to-all-start.1 = ((f32[2,48,128,128]{3,2,0,1:T(8,128)}), f32[2,48,128,128]{3,2,0,1:T(8,128)}, u32[]{:S(2)}, u32[]{:S(2)}) async-start(f32[2,48,128,128]{3,2,0,1:T(8,128)} %select_bitcast_fusion), calls=%async_computation.1 | async-start | bytes 12582912 | tf_op jit(solution)/shard_map/all_to_all | solution.py:63
where the time goes:
time: 337 us; the launch traced here: 335 us
  waiting for transfers between devices  208 us (62%)
  local copies, waits for them, and re-layouts  96.6 us (29%)
  other arithmetic  19 us (6%)
  starting transfers between devices  10.4 us (3%)
    all_to_all x1, waiting for transfers between devices, on_device(): lax.all_to_all(picked, 'gy', split_axis=1, concat_axis=0, tiled=True)  138 us
    all_to_all x1, waiting for transfers between devices, on_device(): lax.all_to_all(outgoing, 'gx', split_axis=1, concat_axis=1, tiled=True)  69.4 us
    rev x1, local copies, waits for them, and re-layouts, spin_patches(): half_turn = jnp.rot90(incoming_patches, 2, axes=(2, 3))  25.7 us
    rev x1, local copies, waits for them, and re-layouts, spin_patches(): last_turn = jnp.rot90(incoming_patches, 3, axes=(2, 3))  17 us
    rev x1, local copies, waits for them, and re-layouts, spin_patches(): first_turn = jnp.rot90(incoming_patches, 1, axes=(2, 3))  15.3 us
    scatter x2, local copies, waits for them, and re-layouts, on_device(): outgoing = outgoing.at[:, mine_place].set(incoming_patches)  12.7 us
    select_n x1, other arithmetic, on_device(): picked = jnp.where(present[None, :, None, None], picked, jnp.float32(0.0))  7.01 us
  transfers between devices with their start and end apart: 2, of which 2 were waited for; matrix products, arithmetic and copies ran while one was open for 0% of the time, Pallas kernels for 0%

commit v1 on v0

--- a/solution.py
+++ b/solution.py
@@ -49,7 +49,10 @@
         jnp.float32,
     )
     outgoing = outgoing.at[:, mine_place].set(incoming_patches)
-    arrived = lax.all_to_all(outgoing, "gx", split_axis=1, concat_axis=1, tiled=True)
+    arrived = jnp.concatenate(
+        lax.all_to_all(jnp.stack(jnp.split(outgoing, lax.axis_size("gx"), axis=1)), "gx", 0, 0),
+        axis=1,
+    )
     arrival = source_group * per_peer + order_rank
     row_ids = jnp.arange(row_count, dtype=jnp.int32)[:, None]
     slot_ids = jnp.arange(capacity, dtype=jnp.int32)[None, :]

time: 337 us -> 348 us (1.033)
  local copies, waits for them, and re-layouts: 96.6 us -> 107 us
    unnamed x7 -> x14, local copies, waits for them, and re-layouts: 2.85 us -> 17.5 us
    reshape x0 -> x1, local copies, waits for them, and re-layouts: none -> 6.28 us  [on_device(): jnp.concatenate(lax.all_to_all(jnp.stack(jnp.split(outgoing, lax.axis_siz...]
    all_to_all x1 -> x0, local copies, waits for them, and re-layouts: 6.28 us -> none  [on_device(): lax.all_to_all(outgoing, 'gx', split_axis=1, concat_axis=1, tiled=True)]
    scatter x2 -> x1, local copies, waits for them, and re-layouts: 12.7 us -> 6.45 us  [on_device(): outgoing = outgoing.at[:, mine_place].set(incoming_patches)]
where the time goes in v1:
time: 348 us; the launch traced here: 345 us
  waiting for transfers between devices  208 us (60%)
  local copies, waits for them, and re-layouts  107 us (31%)
  other arithmetic  19 us (5%)
  starting transfers between devices  10.4 us (3%)
    all_to_all x1, waiting for transfers between devices, on_device(): lax.all_to_all(picked, 'gy', split_axis=1, concat_axis=0, tiled=True)  138 us
    all_to_all x1, waiting for transfers between devices, on_device(): lax.all_to_all(jnp.stack(jnp.split(outgoing, lax.axis_size('gx'), axis=1)...  69.4 us
    rev x1, local copies, waits for them, and re-layouts, spin_patches(): half_turn = jnp.rot90(incoming_patches, 2, axes=(2, 3))  25.7 us
    unnamed x14, local copies, waits for them, and re-layouts  17.5 us
    rev x1, local copies, waits for them, and re-layouts, spin_patches(): last_turn = jnp.rot90(incoming_patches, 3, axes=(2, 3))  17 us
    rev x1, local copies, waits for them, and re-layouts, spin_patches(): first_turn = jnp.rot90(incoming_patches, 1, axes=(2, 3))  15.3 us
    select_n x1, other arithmetic, on_device(): picked = jnp.where(present[None, :, None, None], picked, jnp.float32(0.0))  7.01 us
  transfers between devices with their start and end apart: 2, of which 2 were waited for; matrix products, arithmetic and copies ran while one was open for 0% of the time, Pallas kernels for 0%

profile of v1, /device:TPU:2, one launch (start us, length us, event | category | flops | bytes accessed | tf_op | source)
XLA Modules:
  0.0 345.1 jit_solution(11223330677872682965)
XLA Ops:
  0.0 2.4 copy.26
  2.4 25.7 %rev.17 = f32[2,24,128,128]{3,2,1,0:T(8,128)} reverse(f32[2,24,128,128]{3,2,1,0:T(8,128)} %param.5), dimensions={2,3} | reverse | bytes 6291456 | tf_op jit(solution)/shard_map/jit(rot90)/jit(_flip)/rev | solution.py:9
  28.1 0.0 copy-start.2
  28.1 15.3 %rev.16 = f32[2,24,128,128]{2,3,1,0:T(8,128)} reverse(f32[2,24,128,128]{2,3,1,0:T(8,128)S(1)} %copy.26), dimensions={3} | reverse | bytes 6291456 | tf_op jit(solution)/shard_map/jit(rot90)/jit(_flip)/rev | solution.py:8
  43.4 17.0 %rev.18 = f32[2,24,128,128]{3,2,1,0:T(8,128)} reverse(f32[2,24,128,128]{3,2,1,0:T(8,128)S(1)} %bitcast.68), dimensions={3} | reverse | bytes 6291456 | tf_op jit(solution)/shard_map/jit(rot90)/jit(_flip)/rev | solution.py:10
  60.4 0.0 copy-done.2
  60.4 0.1 broadcast_compare_fusion.2
  60.5 6.2 %fusion.2 = f32[24,2,128,128]{3,2,0,1:T(8,128)S(1)} fusion(f32[2,24,128,128]{3,2,1,0:T(8,128)} %param.5, f32[2,24,128,128]{2,3,1,0:T(8,128)} %rev.16, f32[2,24,128,128]{3,2,1,0:T(8,128)} %rev.17, f32[2,24,128,128]{3,2,1,0:T(8,128)} %rev.18, pred[24]{0:T(512)(128)(4,1)S(1)} %get-tuple-element.12, pred[24]{0:T(512)(128)(4,1)S(1)} %get-tuple-element.11, ...), kind=kLoop, calls=%fused_computation.8 | loop fusion | flops 2359296 | bytes 15728712 | tf_op jit(solution)/shard_map/jit(_where)/select_n | solution.py:12
  66.7 0.0 copy-start
  66.7 0.0 copy-start.1
  66.7 0.2 copy.28
  66.9 0.4 copy-done
  67.4 0.0 copy-done.1
  67.4 0.6 reduce-window.6
  68.0 0.2 slice_reduce_fusion
  68.3 0.1 bitcast_bitcast_fusion
  68.4 0.1 compare_select_fusion
  68.5 3.5 %broadcast_in_dim.88 = f32[2,48,128,128]{3,2,1,0:T(8,128)} broadcast(f32[]{:T(128)} %constant.72.clone.1), dimensions={} | broadcast | bytes 6291460 | tf_op jit(solution)/shard_map/broadcast_in_dim | solution.py:47
  72.0 6.4 %scatter_fusion = f32[2,48,128,128]{3,2,1,0:T(8,128)} fusion(f32[2,48,128,128]{3,2,1,0:T(8,128)} %broadcast_in_dim.88, s32[24]{0:T(128)S(1)} %compare_select_fusion, f32[24,2,128,128]{3,2,1,0:T(8,128)S(1)} %copy.28), kind=kCustom, calls=%fused_computation.1 | custom fusion | bytes 9437280 | tf_op jit(solution)/shard_map/scatter | solution.py:51
  78.4 2.1 fusion.10
  80.5 2.1 fusion.9
  82.6 2.1 fusion.8
  84.7 2.2 fusion.7
  86.8 2.1 fusion.6
  88.9 2.1 fusion.5
  91.0 2.1 fusion.4
  93.1 2.1 fusion.3
  95.2 4.7 %all-to-all-start = ((f32[8,2,6,128,128]{4,3,2,1,0:T(8,128)}), f32[8,2,6,128,128]{4,3,2,1,0:T(8,128)}, u32[]{:S(2)}, u32[]{:S(2)}) async-start(f32[8,2,6,128,128]{4,3,2,1,0:T(8,128)} %fusion.3), calls=%async_computation | async-start | bytes 12582912 | tf_op jit(solution)/shard_map/all_to_all | solution.py:53
  99.9 0.1 iota_add_fusion
  100.0 0.1 add.94
  100.1 0.2 select_reduce_fusion.1
  100.3 69.4 %all-to-all-done = f32[8,2,6,128,128]{4,3,2,1,0:T(8,128)} async-done(((f32[8,2,6,128,128]{4,3,2,1,0:T(8,128)}), f32[8,2,6,128,128]{4,3,2,1,0:T(8,128)}, u32[]{:S(2)}, u32[]{:S(2)}) %all-to-all-start) | async-done | bytes 6291488 | tf_op jit(solution)/shard_map/all_to_all | solution.py:53
  169.7 6.3 %copy.29 = f32[2,8,6,128,128]{4,3,2,1,0:T(8,128)} copy(f32[2,8,6,128,128]{4,3,2,0,1:T(8,128)} %bitcast.13) | data formatting | bytes 12582912 | tf_op jit(solution)/shard_map/reshape | solution.py:52
  176.0 6.4 %gather_fusion = f32[48,2,128,128]{3,2,1,0:T(8,128)} fusion(f32[2,48,128,128]{3,2,1,0:T(8,128)} %bitcast.69, s32[1024]{0:T(1024)S(1)} %pad_clamp_fusion), kind=kCustom, calls=%fused_computation | custom fusion | bytes 12583104 | tf_op jit(solution)/shard_map/jit(_take)/gather | solution.py:64
  182.4 7.0 %select_bitcast_fusion = f32[2,48,128,128]{3,2,0,1:T(8,128)} fusion(f32[48,2,128,128]{3,2,1,0:T(8,128)} %gather_fusion, pred[48]{0:T(512)(128)(4,1)S(1)} %get-tuple-element.14, pred[48]{0:T(512)(128)(4,1)S(1)} %get-tuple-element.13), kind=kLoop, calls=%fused_computation.4 | loop fusion | flops 3145728 | bytes 12583008 | tf_op jit(solution)/shard_map/jit(_where)/select_n | solution.py:65
  189.4 5.7 %all-to-all-start.1 = ((f32[2,48,128,128]{3,2,0,1:T(8,128)}), f32[2,48,128,128]{3,2,0,1:T(8,128)}, u32[]{:S(2)}, u32[]{:S(2)}) async-start(f32[2,48,128,128]{3,2,0,1:T(8,128)} %select_bitcast_fusion), calls=%async_computation.1 | async-start | bytes 12582912 | tf_op jit(solution)/shard_map/all_to_all | solution.py:66
  195.7 138.3 %all-to-all-done.1 = f32[2,48,128,128]{3,2,0,1:T(8,128)} async-done(((f32[2,48,128,128]{3,2,0,1:T(8,128)}), f32[2,48,128,128]{3,2,0,1:T(8,128)}, u32[]{:S(2)}, u32[]{:S(2)}) %all-to-all-start.1) | async-done | bytes 6291488 | tf_op jit(solution)/shard_map/all_to_all | solution.py:66
  334.0 3.2 copy.30
  337.2 0.8 select_reduce_fusion
  338.0 0.1 broadcast_multiply_fusion
  338.1 3.2 copy.31
  341.3 3.7 %fusion = f32[8,1,12,128,128]{4,3,2,0,1:T(8,128)} fusion(f32[4,2,12,128,128]{4,3,2,1,0:T(8,128)S(1)} %copy.31, f32[12,128,128]{2,1,0:T(8,128)S(1)} %broadcast_multiply_fusion, pred[12]{0:T(512)(128)(4,1)S(1)} %iota_compare_fusion.2), kind=kLoop, calls=%fused_computation.3 | loop fusion | flops 3145728 | bytes 13369356 | tf_op jit(solution)/shard_map/sub | solution.py:69
  (12 shorter events, 0.2 us)
Async XLA Ops:
  28.1 32.4 %copy-start.2 = (s32[192]{0:T(256)S(1)}, s32[192]{0:T(256)}, u32[]{:S(2)}) copy-start(s32[192]{0:T(256)} %param.8) | copy-start | bytes 2308
  66.7 0.7 copy-start
  66.7 0.7 copy-start.1
  95.2 74.5 %all-to-all-start = ((f32[8,2,6,128,128]{4,3,2,1,0:T(8,128)}), f32[8,2,6,128,128]{4,3,2,1,0:T(8,128)}, u32[]{:S(2)}, u32[]{:S(2)}) async-start(f32[8,2,6,128,128]{4,3,2,1,0:T(8,128)} %fusion.3), calls=%async_computation | async-start | bytes 12582912 | tf_op jit(solution)/shard_map/all_to_all | solution.py:53
  189.4 144.6 %all-to-all-start.1 = ((f32[2,48,128,128]{3,2,0,1:T(8,128)}), f32[2,48,128,128]{3,2,0,1:T(8,128)}, u32[]{:S(2)}, u32[]{:S(2)}) async-start(f32[2,48,128,128]{3,2,0,1:T(8,128)} %select_bitcast_fusion), calls=%async_computation.1 | async-start | bytes 12582912 | tf_op jit(solution)/shard_map/all_to_all | solution.py:66
